TPU v7x, 32 devices: a whole 2x2x4 slice. The times are simulated.
32 devices in a mesh: ctx: 8 (over z, x), tp: 4 (over y, core).
Axes of the slice: x: 2, y: 2, z: 4, core: 2. Of those that a mesh axis runs over, the one named last changes fastest.
Arguments:
- queries: bfloat16 [2048, 8192], P('ctx', 'tp'), may hold values from -8 to 8
- keys: bfloat16 [2048, 1024], P('ctx'), may hold values from -7 to 7
- values: bfloat16 [2048, 1024], P('ctx'), may hold values from -6 to 6
- out_weight: bfloat16 [8192, 4096], P('tp'), may hold values from -0.25 to 0.25
- block_order: int32 [16], P('ctx'), may hold values from 0 to 15, each once
Outputs:
- projected: bfloat16 [2048, 4096], P('ctx', 'tp')
Inputs may be any that keep to these rules, and one draw needn't show every extreme that they name: `block_order`: every sequence block appears exactly once.
All inputs are finite; a program needn't handle non-finite values.
Results may differ from a plain program's by a relative error of at most 0.015.
Values may be sent and summed in bfloat16 or wider, within the bound.
A program may use at most 64 MiB of HBM per device.

v0:
```python
import math

import jax
import jax.numpy as jnp
from jax import lax
from jax.sharding import PartitionSpec as P

QUERY_HEADS = 64
KEY_VALUE_HEADS = 8
HEAD_SIZE = 128


def shards(queries, keys, values, out_weight, block_order):
    tok_rows = queries.shape[0]
    block_len = tok_rows // 2
    heads_dev = queries.shape[1] // HEAD_SIZE
    group_size = QUERY_HEADS // KEY_VALUE_HEADS
    kv_heads = max(1, heads_dev // group_size)
    head_group = heads_dev // kv_heads
    whole_order = lax.all_gather(block_order, "ctx", axis=0, tiled=True)
    offsets = jnp.arange(block_len, dtype=jnp.int32)
    all_pos = (whole_order[:, None] * block_len + offsets[None, :]).reshape(-1)
    local_pos = (block_order[:, None] * block_len + offsets[None, :]).reshape(-1)
    first_head = lax.axis_index("tp") * heads_dev // group_size
    column_start = first_head * HEAD_SIZE
    own_keys = lax.dynamic_slice_in_dim(keys, column_start, kv_heads * HEAD_SIZE, 1)
    own_values = lax.dynamic_slice_in_dim(values, column_start, kv_heads * HEAD_SIZE, 1)
    scale = 1.0 / math.sqrt(HEAD_SIZE)
    query_heads = queries.reshape(tok_rows, kv_heads, head_group, HEAD_SIZE)
    last_pos = jnp.max(local_pos)

    def update(state, key_block, value_block, pos_block):
        run_max, run_sum, accum = state
        keyed = key_block.reshape(-1, kv_heads, HEAD_SIZE)
        valued = value_block.reshape(-1, kv_heads, HEAD_SIZE)
        scores = (
            jnp.einsum("tkgd,skd->kgts", query_heads, keyed, preferred_element_type=jnp.float32)
            * scale
        )
        visible = pos_block[None, None, None, :] <= local_pos[None, None, :, None]
        new_max = jnp.maximum(run_max, jnp.max(jnp.where(visible, scores, -1e30), axis=-1))
        weights = jnp.where(visible, jnp.exp(scores - new_max[..., None]), 0.0)
        factor = jnp.exp(run_max - new_max)
        run_sum = run_sum * factor + jnp.sum(weights, axis=-1)
        spread = jnp.transpose(factor, (2, 0, 1))[..., None]
        accum = accum * spread + jnp.einsum(
            "kgts,skd->tkgd",
            weights.astype(jnp.bfloat16),
            valued,
            preferred_element_type=jnp.float32,
        )
        return (new_max, run_sum, accum)

    start_state = (
        jnp.full((kv_heads, head_group, tok_rows), -1e30, jnp.float32),
        jnp.zeros((kv_heads, head_group, tok_rows), jnp.float32),
        jnp.zeros((tok_rows, kv_heads, head_group, HEAD_SIZE), jnp.float32),
    )
    piece_keys = lax.all_gather(own_keys, "ctx", axis=0, tiled=True)
    piece_values = lax.all_gather(own_values, "ctx", axis=0, tiled=True)
    rows = piece_keys.shape[0]
    step_rows = math.gcd(rows, 512)

    def advance(carry, blocks):
        result = lax.cond(
            jnp.min(blocks[2]) <= last_pos,
            lambda inner: update(inner, blocks[0], blocks[1], blocks[2]),
            lambda inner: inner,
            carry,
        )
        return (result, None)

    stacked = (
        piece_keys.reshape(rows // step_rows, step_rows, -1),
        piece_values.reshape(rows // step_rows, step_rows, -1),
        all_pos.reshape(rows // step_rows, step_rows),
    )
    result, _ = lax.scan(advance, start_state, stacked)
    run_max, run_sum, accum = result
    totals = jnp.transpose(run_sum, (2, 0, 1))[..., None]
    attended = (accum / totals).reshape(tok_rows, heads_dev * HEAD_SIZE).astype(jnp.bfloat16)
    summed = lax.psum_scatter(
        lax.dot_general(
            out_weight, attended, (((0,), (1,)), ((), ())), preferred_element_type=jnp.float32
        ).astype(jnp.bfloat16),
        "tp",
        scatter_dimension=0,
        tiled=True,
    ).astype(jnp.float32)
    return summed.T.astype(jnp.bfloat16)


def solution(mesh):
    in_specs = (P("ctx", "tp"), P("ctx", None), P("ctx", None), P("tp", None), P("ctx"))
    out_specs = P("ctx", "tp")
    return jax.shard_map(shards, mesh=mesh, in_specs=in_specs, out_specs=out_specs, check_vma=False)
```

profile of v0, /device:TPU:0, one launch (start us, length us, event | category | flops | bytes accessed | tf_op | source)
XLA Modules:
  0.0 191.4 jit_solution(12870223693085715618)
XLA Ops:
  6.5 1.0 copy-done
  7.6 0.7 constant_dynamic-slice_fusion.4
  8.2 0.0 all-gather.3.cloned.1.call-update
  8.3 0.0 all-gather.5.cloned.1.call-start
  8.3 1.6 constant_dynamic-slice_fusion.3
  9.9 0.0 all-gather.5.cloned.1.call-update
  9.9 0.0 reduce-scatter.2.cloned.1.call-start
  10.0 1.3 dynamic-slice
  12.0 0.9 dynamic-update-slice
  12.8 13.1 %all-reduce = s32[16]{0:T(128)S(1)} all-reduce(s32[16]{0:T(128)S(1)} %dynamic-update-slice), channel_id=1, replica_groups=mesh['ctx'=8,'tp'=4] {'ctx'}, use_global_device_ids=true, to_apply=%add | all-reduce | flops 16 | bytes 128
  26.0 0.1 add.57
  26.1 1.5 copy.24
  27.5 0.7 copy.26
  28.2 0.7 broadcast_multiply_fusion
  28.9 0.7 add_reduce_fusion
  29.6 0.1 broadcast_bitcast_fusion
  29.7 22.8 %all-gather.3.cloned.1.call-done = bf16[2048,256]{1,0:T(8,128)(2,1)} async-done(((bf16[256,256]{1,0:T(8,128)(2,1)}), bf16[2048,256]{1,0:T(8,128)(2,1)}) %all-gather.3.cloned.1.call-update) | async-done | bytes 1048592 | tf_op jit(solution)/shard_map/all_gather | solution.py:59
  52.5 1.5 copy.25
  54.0 39.6 %all-gather.5.cloned.1.call-done = bf16[2048,256]{1,0:T(8,128)(2,1)} async-done(((bf16[256,256]{1,0:T(8,128)(2,1)}), bf16[2048,256]{1,0:T(8,128)(2,1)}) %all-gather.5.cloned.1.call-update) | async-done | bytes 1048592 | tf_op jit(solution)/shard_map/all_gather | solution.py:60
  93.7 2.3 %copy.27 = bf16[4,512,256]{1,2,0:T(8,128)(2,1)} copy(bf16[4,512,256]{2,1,0:T(8,128)(2,1)} %bitcast.58) | data formatting | bytes 2097152
  95.9 1.6 broadcast_in_dim.44
  97.5 43.6 %while.15 = (s32[]{:T(128)}, f32[2,8,256]{2,1,0:T(8,128)S(1)}, f32[2,8,256]{2,1,0:T(8,128)S(1)}, f32[256,2,8,128]{3,0,2,1:T(8,128)}, s32[4,512]{1,0:T(4,128)S(1)...) while((s32[]{:T(128)}, f32[2,8,256]{2,1,0:T(8,128)S(1)}, ...), condition=%wide.region_7.8_spmd.clone, body=%wide.region_1.7_spmd.clone.sunk | while | flops 1098003200 | bytes 49555792 | solution.py:78
  97.5 0.6 fusion.23
  99.4 9.0 %conditional.3 = ((f32[2,8,256]{2,1,0:T(8,128)S(1)}, f32[2,8,256]{2,1,0:T(8,128)S(1)}, f32[256,2,8,128]{3,0,2,1:T(8,128)})) conditional(s32[]{:T(128)} %convert_element_type.40, (f32[2,8,256]{2,1,0:T(8,128)S(1)}, f32[2,8,256]{2,1,0:T(8,128)S(1)}, f32[256,2,8,128]{3,0,2,1:T(8,128)}) %tuple.45, (s32[1,512]{1,0:T(1,128)S(1)}, s32[2]{0:T(128)S(1)}, ...), branch_computations={%region_3.3_spmd, %region_4.6_spmd} | conditional | flops 1098002688 | bytes 49550436 | solution.py:65
  99.4 0.1 add_bitcast_fusion
  99.5 0.1 broadcast_compare_fusion
  99.6 1.0 constant_dynamic-slice_fusion
  100.6 0.0 copy-start.1
  100.6 1.5 fusion.2
  102.2 1.7 fusion.6
  103.9 3.2 %bitcast_add_fusion = f32[256,2,8,128]{3,0,2,1:T(8,128)S(1)} fusion(f32[256,2,8,128]{3,0,2,1:T(8,128)S(1)} %copy-done.1, bf16[512,2,128,1]{0,2,3,1:T(8,128)(2,1)S(1)} %bitcast.54, f32[2,512,256,8]{2,1,3,0:T(8,128)S(1)} %get-tuple-element.228, f32[2,8,256]{2,1,0:T(8,128)S(1)} %get-tuple-element.305, pred[256,512]{0,1:T(8,128)(4,1)S(1)} %broadcast_compare_fusion, ...), kind=kOutput, calls=%fused_computation.10 | convolution fusion | flops 546308096 | bytes 13008896 | tf_op jit(solution)/shard_map/while/body/eval_jaxpr/cond/branch_1_fun/kgts,skd->tkgd/dot_general | solution.py:46
  107.1 1.3 copy-done.2
  108.4 0.6 fusion.23
  110.3 9.0 %conditional.3 = ((f32[2,8,256]{2,1,0:T(8,128)S(1)}, f32[2,8,256]{2,1,0:T(8,128)S(1)}, f32[256,2,8,128]{3,0,2,1:T(8,128)})) conditional(s32[]{:T(128)} %convert_element_type.40, (f32[2,8,256]{2,1,0:T(8,128)S(1)}, f32[2,8,256]{2,1,0:T(8,128)S(1)}, f32[256,2,8,128]{3,0,2,1:T(8,128)}) %tuple.45, (s32[1,512]{1,0:T(1,128)S(1)}, s32[2]{0:T(128)S(1)}, ...), branch_computations={%region_3.3_spmd, %region_4.6_spmd} | conditional | flops 1098002688 | bytes 49550436 | solution.py:65
  110.3 0.1 add_bitcast_fusion
  110.3 0.1 broadcast_compare_fusion
  110.5 1.0 constant_dynamic-slice_fusion
  111.5 1.5 fusion.2
  113.0 1.7 fusion.6
  114.8 3.2 %bitcast_add_fusion = f32[256,2,8,128]{3,0,2,1:T(8,128)S(1)} fusion(f32[256,2,8,128]{3,0,2,1:T(8,128)S(1)} %copy-done.1, bf16[512,2,128,1]{0,2,3,1:T(8,128)(2,1)S(1)} %bitcast.54, f32[2,512,256,8]{2,1,3,0:T(8,128)S(1)} %get-tuple-element.228, f32[2,8,256]{2,1,0:T(8,128)S(1)} %get-tuple-element.305, pred[256,512]{0,1:T(8,128)(4,1)S(1)} %broadcast_compare_fusion, ...), kind=kOutput, calls=%fused_computation.10 | convolution fusion | flops 546308096 | bytes 13008896 | tf_op jit(solution)/shard_map/while/body/eval_jaxpr/cond/branch_1_fun/kgts,skd->tkgd/dot_general | solution.py:46
  117.9 1.3 copy-done.2
  119.3 0.6 fusion.23
  121.1 9.0 %conditional.3 = ((f32[2,8,256]{2,1,0:T(8,128)S(1)}, f32[2,8,256]{2,1,0:T(8,128)S(1)}, f32[256,2,8,128]{3,0,2,1:T(8,128)})) conditional(s32[]{:T(128)} %convert_element_type.40, (f32[2,8,256]{2,1,0:T(8,128)S(1)}, f32[2,8,256]{2,1,0:T(8,128)S(1)}, f32[256,2,8,128]{3,0,2,1:T(8,128)}) %tuple.45, (s32[1,512]{1,0:T(1,128)S(1)}, s32[2]{0:T(128)S(1)}, ...), branch_computations={%region_3.3_spmd, %region_4.6_spmd} | conditional | flops 1098002688 | bytes 49550436 | solution.py:65
  121.2 0.1 add_bitcast_fusion
  121.2 0.1 broadcast_compare_fusion
  121.4 1.0 constant_dynamic-slice_fusion
  122.4 1.5 fusion.2
  123.9 1.7 fusion.6
  125.7 3.2 %bitcast_add_fusion = f32[256,2,8,128]{3,0,2,1:T(8,128)S(1)} fusion(f32[256,2,8,128]{3,0,2,1:T(8,128)S(1)} %copy-done.1, bf16[512,2,128,1]{0,2,3,1:T(8,128)(2,1)S(1)} %bitcast.54, f32[2,512,256,8]{2,1,3,0:T(8,128)S(1)} %get-tuple-element.228, f32[2,8,256]{2,1,0:T(8,128)S(1)} %get-tuple-element.305, pred[256,512]{0,1:T(8,128)(4,1)S(1)} %broadcast_compare_fusion, ...), kind=kOutput, calls=%fused_computation.10 | convolution fusion | flops 546308096 | bytes 13008896 | tf_op jit(solution)/shard_map/while/body/eval_jaxpr/cond/branch_1_fun/kgts,skd->tkgd/dot_general | solution.py:46
  128.8 1.3 copy-done.2
  130.2 0.6 fusion.23
  132.0 9.0 %conditional.3 = ((f32[2,8,256]{2,1,0:T(8,128)S(1)}, f32[2,8,256]{2,1,0:T(8,128)S(1)}, f32[256,2,8,128]{3,0,2,1:T(8,128)})) conditional(s32[]{:T(128)} %convert_element_type.40, (f32[2,8,256]{2,1,0:T(8,128)S(1)}, f32[2,8,256]{2,1,0:T(8,128)S(1)}, f32[256,2,8,128]{3,0,2,1:T(8,128)}) %tuple.45, (s32[1,512]{1,0:T(1,128)S(1)}, s32[2]{0:T(128)S(1)}, ...), branch_computations={%region_3.3_spmd, %region_4.6_spmd} | conditional | flops 1098002688 | bytes 49550436 | solution.py:65
  132.1 0.1 add_bitcast_fusion
  132.1 0.1 broadcast_compare_fusion
  132.3 1.0 constant_dynamic-slice_fusion
  133.3 1.5 fusion.2
  134.8 1.7 fusion.6
  136.6 3.2 %bitcast_add_fusion = f32[256,2,8,128]{3,0,2,1:T(8,128)S(1)} fusion(f32[256,2,8,128]{3,0,2,1:T(8,128)S(1)} %copy-done.1, bf16[512,2,128,1]{0,2,3,1:T(8,128)(2,1)S(1)} %bitcast.54, f32[2,512,256,8]{2,1,3,0:T(8,128)S(1)} %get-tuple-element.228, f32[2,8,256]{2,1,0:T(8,128)S(1)} %get-tuple-element.305, pred[256,512]{0,1:T(8,128)(4,1)S(1)} %broadcast_compare_fusion, ...), kind=kOutput, calls=%fused_computation.10 | convolution fusion | flops 546308096 | bytes 13008896 | tf_op jit(solution)/shard_map/while/body/eval_jaxpr/cond/branch_1_fun/kgts,skd->tkgd/dot_general | solution.py:46
  139.7 1.3 copy-done.2
  141.1 1.9 %copy.28 = f32[256,2,8,128]{0,3,2,1:T(8,128)S(1)} copy(f32[256,2,8,128]{3,0,2,1:T(8,128)} %get-tuple-element.142) | data formatting | bytes 4194304 | tf_op jit(solution)/shard_map/while | solution.py:78
  143.0 0.2 divide_convert_fusion
  143.2 11.6 %fusion.15 = bf16[4096,256]{0,1:T(8,128)(2,1)} fusion(bf16[256,2048]{0,1:T(8,128)(2,1)S(1)} %bitcast.55, bf16[2048,4096]{1,0:T(8,128)(2,1)} %param.12), kind=kOutput, calls=%fused_computation.22 | convolution fusion | flops 4296015872 | bytes 19922944 | tf_op jit(solution)/shard_map/dot_general | solution.py:83
  154.8 0.0 reduce-scatter.2.cloned.1.call-update
  154.8 30.1 %reduce-scatter.2.cloned.1.call-done = bf16[1024,256]{0,1:T(8,128)(2,1)} async-done(((bf16[4096,256]{0,1:T(8,128)(2,1)}), bf16[1024,256]{0,1:T(8,128)(2,1)}) %reduce-scatter.2.cloned.1.call-update) | async-done | bytes 524304 | tf_op jit(solution)/shard_map/reduce_scatter | solution.py:82
  (35 shorter events, 0.2 us)
Async XLA Ops:
  6.5 1.0 copy-start
  6.5 46.0 %all-gather.3.cloned.1.call-start = ((), (), s32[]{:S(2)}) async-start(), calls=%async_computation.1 | async-start | bytes 1179648 | tf_op jit(solution)/shard_map/all_gather | solution.py:59
  8.3 85.4 %all-gather.5.cloned.1.call-start = ((), (), s32[]{:S(2)}) async-start(), calls=%async_computation.2 | async-start | bytes 1179648 | tf_op jit(solution)/shard_map/all_gather | solution.py:60
  9.9 174.9 %reduce-scatter.2.cloned.1.call-start = ((), (), s32[]{:S(2)}) async-start(), calls=%async_computation.3 | async-start | bytes 2621440 | tf_op jit(solution)/shard_map/reduce_scatter | solution.py:82
  100.6 3.3 %copy-start.1 = (f32[256,2,8,128]{3,0,2,1:T(8,128)S(1)}, f32[256,2,8,128]{3,0,2,1:T(8,128)}, u32[]{:S(2)}) copy-start(f32[256,2,8,128]{3,0,2,1:T(8,128)} %get-tuple-element.124) | copy-start | bytes 6291460 | tf_op jit(solution)/shard_map/while/body/eval_jaxpr/cond
  107.0 1.3 copy-start.2
  111.5 3.3 %copy-start.1 = (f32[256,2,8,128]{3,0,2,1:T(8,128)S(1)}, f32[256,2,8,128]{3,0,2,1:T(8,128)}, u32[]{:S(2)}) copy-start(f32[256,2,8,128]{3,0,2,1:T(8,128)} %get-tuple-element.124) | copy-start | bytes 6291460 | tf_op jit(solution)/shard_map/while/body/eval_jaxpr/cond
  117.9 1.3 copy-start.2
  122.4 3.3 %copy-start.1 = (f32[256,2,8,128]{3,0,2,1:T(8,128)S(1)}, f32[256,2,8,128]{3,0,2,1:T(8,128)}, u32[]{:S(2)}) copy-start(f32[256,2,8,128]{3,0,2,1:T(8,128)} %get-tuple-element.124) | copy-start | bytes 6291460 | tf_op jit(solution)/shard_map/while/body/eval_jaxpr/cond
  128.8 1.3 copy-start.2
  133.3 3.3 %copy-start.1 = (f32[256,2,8,128]{3,0,2,1:T(8,128)S(1)}, f32[256,2,8,128]{3,0,2,1:T(8,128)}, u32[]{:S(2)}) copy-start(f32[256,2,8,128]{3,0,2,1:T(8,128)} %get-tuple-element.124) | copy-start | bytes 6291460 | tf_op jit(solution)/shard_map/while/body/eval_jaxpr/cond
  139.7 1.3 copy-start.2
Sparse Core Ops, SparseCore 0:
  9.5 43.0 all-gather.2
  54.6 38.9 all-gather.4
  154.9 29.9 reduce-scatter.1
where the time goes:
time: 192 us; the launch traced here: 191 us
  waiting for transfers between devices  92.6 us (48%)
  matrix products  30.2 us (16%)
  local copies, waits for them, and re-layouts  24.3 us (13%)
  between operations  13.9 us (7%)
  blocking collectives  13.1 us (7%)
  other arithmetic  11.9 us (6%)
  loops' own time  5.26 us (3%)
    all_gather x1, waiting for transfers between devices, shards(): piece_values = lax.all_gather(own_values, 'ctx', axis=0, tiled=True)  39.6 us
    reduce_scatter x1, waiting for transfers between devices, shards(): lax.psum_scatter(lax.dot_general(out_weight, attended, (((0,), (1,)), (()...  30.1 us
    all_gather x1, waiting for transfers between devices, shards(): piece_keys = lax.all_gather(own_keys, 'ctx', axis=0, tiled=True)  22.8 us
    unnamed x1, blocking collectives  13.1 us
    dot_general x4, matrix products, update(): jnp.einsum('kgts,skd->tkgd', weights.astype(jnp.bfloat16), valued, prefer...  12.6 us
    dot_general x1, matrix products, shards(): lax.dot_general(out_weight, attended, (((0,), (1,)), ((), ())), preferred...  11.6 us
    unnamed x10, local copies, waits for them, and re-layouts  9.18 us
    reduce_sum x4, other arithmetic, update(): run_sum = run_sum * factor + jnp.sum(weights, axis=-1)  6.79 us
  transfers between devices with their start and end apart: 3, of which 3 were waited for; matrix products, arithmetic and copies ran while one was open for 5% of the time, Pallas kernels for 0%

commit v1 on v0

v1 whole, which is shorter than its diff:
```python
import functools
import math

import jax
import jax.numpy as jnp
from jax import lax
from jax.experimental import pallas as pl
from jax.experimental.pallas import tpu as pltpu
from jax.sharding import PartitionSpec as P

QUERY_HEADS = 64
KEY_VALUE_HEADS = 8
HEAD_SIZE = 128
MESH = pl.DeviceIdType.MESH
NT = (((1,), (1,)), ((), ()))


def kernel(dims, q_hbm, k_hbm, v_hbm, w_hbm, order, o_ref, q, w, kv, tile, orders, mask, eye, scores,
           att, pair_out, pair_in, far_out, far_in, load_sem, order_send, order_recv, send, recv,
           pair_send, pair_recv, far_send, far_recv):
    n, tp, rows, heads, kv_heads, unit, wide = dims
    line, groups = n // 2, tp // 2
    tokens = n * rows
    blocks = rows // 128
    per_kv = heads // kv_heads
    me, t = lax.axis_index("ctx"), lax.axis_index("tp")
    a, b = me // 2, lax.rem(me, 2)
    y, c = t // 2, lax.rem(t, 2)
    other = 1 - b
    partner = (me, y * 2 + 1 - c)

    def far(i):
        return lax.rem(y + i, groups)

    first = t * heads // (QUERY_HEADS // KEY_VALUE_HEADS)
    own = pl.ds(pl.multiple_of(me * rows, 128), rows)
    loads = []
    for p in range(2 * kv_heads):
        src = v_hbm if p % 2 else k_hbm
        cols = pl.ds(pl.multiple_of((first + p // 2) * HEAD_SIZE, 128), HEAD_SIZE)
        loads.append(pltpu.make_async_copy(src.at[:, cols], kv.at[p, own, :], load_sem.at[p]))
        loads[-1].start()
    q_load = pltpu.make_async_copy(q_hbm, q, load_sem.at[2 * kv_heads])
    w_load = pltpu.make_async_copy(w_hbm, w, load_sem.at[2 * kv_heads + 1])
    q_load.start()
    w_load.start()
    for i in range(blocks):
        tile[pl.ds(i, 1), :] = jnp.full((1, 128), order[i], jnp.int32)

    barrier = pltpu.get_barrier_semaphore()
    for d in range(1, n):
        pl.semaphore_signal(barrier, inc=1, device_id=(lax.rem(me + d, n), t), device_id_type=MESH)
    pl.semaphore_signal(barrier, inc=1, device_id=partner, device_id_type=MESH)
    for i in range(1, groups):
        pl.semaphore_signal(barrier, inc=1, device_id=(me, far(i) * 2 + c), device_id_type=MESH)
    pl.semaphore_wait(barrier, n - 1 + 1 + groups - 1)

    def order_copy(d, src_dev, target):
        return pltpu.make_async_remote_copy(
            src_ref=tile, dst_ref=orders.at[src_dev], send_sem=order_send.at[d],
            recv_sem=order_recv.at[d], device_id=(target, t), device_id_type=MESH)

    def piece(p, block, way, target):
        at = pl.ds(pl.multiple_of(block * rows, 128), rows)
        return pltpu.make_async_remote_copy(
            src_ref=kv.at[p, at, :], dst_ref=kv.at[p, at, :], send_sem=send.at[p, block, way],
            recv_sem=recv.at[p, block], device_id=(target, t), device_id_type=MESH)

    def guarded(cond, act):
        pl.when(cond)(act)

    def open_line(p):
        guarded(a + 1 < line, lambda: piece(p, me, 0, me + 2).start())
        guarded(a > 0, lambda: piece(p, me, 1, me - 2).start())
        piece(p, me, 2, a * 2 + other).start()

    def open_crossed(p):
        blk = a * 2 + other
        piece(p, blk, 2, blk).wait_recv()
        guarded(a + 1 < line, lambda: piece(p, blk, 0, me + 2).start())
        guarded(a > 0, lambda: piece(p, blk, 1, me - 2).start())

    def relay(p, s, side, crossing):
        low, high = (a - s) * 2 + side, (a + s) * 2 + side

        @pl.when(a - s >= 0)
        def _():
            piece(p, low, 0, me).wait_recv()
            guarded(a + 1 < line, lambda: piece(p, low, 0, me + 2).start())
            if crossing:
                piece(p, low, 2, a * 2 + other).start()

        @pl.when(a + s < line)
        def _():
            piece(p, high, 1, me).wait_recv()
            guarded(a > 0, lambda: piece(p, high, 1, me - 2).start())
            if crossing:
                piece(p, high, 2, a * 2 + other).start()

    def step(h, s):
        relay(2 * h, s, b, True)
        relay(2 * h + 1, s, b, False)
        relay(2 * h + 1, s, other, False)

    def finish(h):
        def body(i, _):
            piece(2 * h, i * 2 + other, 2, me).wait_recv()
            return 0
        lax.fori_loop(0, line, body, 0)

    for h in range(kv_heads):
        for p in (2 * h, 2 * h + 1):
            loads[p].wait()
            open_line(p)
        if h == 0:
            for d in range(1, n):
                order_copy(d, me, lax.rem(me + d, n)).start()
    orders[pl.ds(me, 1)] = tile[...][None]
    row = lax.broadcasted_iota(jnp.int32, (128, 128), 0)
    col = lax.broadcasted_iota(jnp.int32, (128, 128), 1)
    eye[...] = (row == col).astype(jnp.bfloat16)
    open_crossed(1)

    for d in range(1, n):
        order_copy(d, lax.rem(me + n - d, n), me).wait_recv()

    def build(i, _):
        for j in range(blocks):
            kpos = orders[pl.ds(i, 1), j:j + 1, :][0] * 128 + row
            for g in range(blocks):
                qpos = tile[g:g + 1, :] * 128 + col
                at = pl.ds(pl.multiple_of(i * rows + j * 128, 128), 128)
                mask[g, at, :] = jnp.where(kpos <= qpos, 0.0, -1e30).astype(jnp.bfloat16)
        return 0
    lax.fori_loop(0, n, build, 0)

    for s in range(1, line):
        step(0, s)
    finish(0)
    q_load.wait()

    chunk = tokens // 4
    factor = math.log2(math.e) / math.sqrt(HEAD_SIZE)
    ones = jnp.ones((chunk, 128), jnp.bfloat16)
    per_block = per_kv // unit

    def attend(h, g, u):
        at = pl.ds(pl.multiple_of(g * 128, 128), 128)
        def head_cols(k):
            return pl.ds(pl.multiple_of((h * per_kv + u * unit + k) * HEAD_SIZE, 128), HEAD_SIZE)
        e = eye[...]
        qa = jnp.concatenate(
            [jnp.concatenate([q[at, head_cols(k)], e], axis=1) for k in range(unit)], axis=0)
        top = None
        for i in range(4):
            ks = pl.ds(i * chunk, chunk)
            ka = jnp.concatenate([kv[2 * h, ks, :], mask[g, ks, :]], axis=1)
            s = lax.dot_general(qa, ka, NT, preferred_element_type=jnp.float32)
            scores[:, ks] = s
            for j in range(0, chunk, 128):
                part = s[:, j:j + 128]
                top = part if top is None else jnp.maximum(top, part)
        top = jnp.max(top, axis=1, keepdims=True)
        acc = None
        for i in range(4):
            ks = pl.ds(i * chunk, chunk)
            weight = jnp.exp2((scores[:, ks] - top) * factor).astype(jnp.bfloat16)
            va = jnp.concatenate([kv[2 * h + 1, ks, :], ones], axis=1)
            part = jnp.dot(weight, va, preferred_element_type=jnp.float32)
            acc = part if acc is None else acc + part
        res = (acc[:, :128] / acc[:, 128:]).astype(jnp.bfloat16)
        for k in range(unit):
            att[at, head_cols(k)] = res[k * 128:(k + 1) * 128]

    total = blocks * per_block
    for h in range(kv_heads):
        def body(i, _):
            attend(h, i // per_block, lax.rem(i, per_block))
            if h + 1 < kv_heads:
                guarded(i == 0, lambda: open_crossed(2 * h + 3))
                guarded(jnp.logical_and(i > 0, i < line), lambda: step(h + 1, i))
            return 0
        lax.fori_loop(0, total, body, 0)
        if h + 1 < kv_heads:
            for s in range(total, line):
                step(h + 1, s)
            finish(h + 1)

    quarter = o_ref.shape[1]
    parts = quarter // wide
    w_load.wait()

    def product(group, core, j):
        cols = pl.ds(pl.multiple_of((group * 2 + core) * quarter + j * wide, 128), wide)
        return jnp.dot(att[...], w[:, cols], preferred_element_type=jnp.float32)

    def pair_copy(i, j):
        return pltpu.make_async_remote_copy(
            src_ref=pair_out.at[i, j], dst_ref=pair_in.at[i, j], send_sem=pair_send.at[i, j],
            recv_sem=pair_recv.at[i, j], device_id=partner, device_id_type=MESH)

    def far_copy(i, j):
        return pltpu.make_async_remote_copy(
            src_ref=far_out.at[i, j], dst_ref=far_in.at[i, j], send_sem=far_send.at[i, j],
            recv_sem=far_recv.at[i, j], device_id=(me, far(i) * 2 + c), device_id_type=MESH)

    def far_step(k, _):
        i, j = 1 + k // parts, lax.rem(k, parts)
        pair_out[i, j] = product(far(i), 1 - c, j).astype(jnp.bfloat16)
        pair_copy(i, j).start()
        mine = product(far(i), c, j)
        pair_copy(i, j).wait_recv()
        far_out[i, j] = (mine + pair_in[i, j].astype(jnp.float32)).astype(jnp.bfloat16)
        far_copy(i, j).start()
        return 0
    lax.fori_loop(0, (groups - 1) * parts, far_step, 0)

    def near_step(j, _):
        pair_out[0, j] = product(y, 1 - c, j).astype(jnp.bfloat16)
        pair_copy(0, j).start()
        far_out[0, j] = product(y, c, j).astype(jnp.bfloat16)
        return 0
    lax.fori_loop(0, parts, near_step, 0)

    def close_step(j, _):
        pair_copy(0, j).wait_recv()
        res = far_out[0, j].astype(jnp.float32) + pair_in[0, j].astype(jnp.float32)
        for i in range(1, groups):
            far_copy(i, j).wait_recv()
            res = res + far_in[i, j].astype(jnp.float32)
        o_ref[:, pl.ds(pl.multiple_of(j * wide, 128), wide)] = res.astype(jnp.bfloat16)
        return 0
    lax.fori_loop(0, parts, close_step, 0)

    for d in range(1, n):
        order_copy(d, me, lax.rem(me + d, n)).wait_send()

    def drain(i, _):
        for p in range(2 * kv_heads):
            for side, tags in ((b, True), (other, p % 2 == 1)):
                blk = i * 2 + side
                if tags:
                    guarded(jnp.logical_and(a + 1 < line, i <= a),
                            lambda: piece(p, blk, 0, me + 2).wait_send())
                    guarded(jnp.logical_and(a > 0, i >= a),
                            lambda: piece(p, blk, 1, me - 2).wait_send())
            if p % 2 == 0:
                piece(p, i * 2 + b, 2, a * 2 + other).wait_send()
            else:
                guarded(i == a, lambda: piece(p, me, 2, a * 2 + other).wait_send())
        return 0
    lax.fori_loop(0, line, drain, 0)

    def drain_out(j, _):
        for i in range(groups):
            pair_copy(i, j).wait_send()
            if i:
                far_copy(i, j).wait_send()
        return 0
    lax.fori_loop(0, parts, drain_out, 0)


def shards(n, tp, queries, keys, values, out_weight, block_order):
    rows = queries.shape[0]
    heads = queries.shape[1] // HEAD_SIZE
    group = QUERY_HEADS // KEY_VALUE_HEADS
    kv_heads = max(1, heads // group)
    unit = min(2, heads // kv_heads)
    quarter = out_weight.shape[1] // tp
    wide = min(256, quarter)
    parts, groups, tokens, blocks = quarter // wide, tp // 2, n * rows, rows // 128
    dims = (n, tp, rows, heads, kv_heads, unit, wide)
    any_space = pl.BlockSpec(memory_space=pl.ANY)
    dma = pltpu.SemaphoreType.DMA
    bf16 = jnp.bfloat16
    swap = pltpu.VMEM((groups, parts, rows, wide), bf16)
    return pl.pallas_call(
        functools.partial(kernel, dims),
        out_shape=jax.ShapeDtypeStruct((rows, quarter), bf16),
        in_specs=[any_space] * 4 + [pl.BlockSpec(memory_space=pltpu.SMEM)],
        out_specs=pl.BlockSpec(memory_space=pltpu.VMEM),
        scratch_shapes=[
            pltpu.VMEM(queries.shape, bf16),
            pltpu.VMEM(out_weight.shape, bf16),
            pltpu.VMEM((2 * kv_heads, tokens, HEAD_SIZE), bf16),
            pltpu.VMEM((8, 128), jnp.int32),
            pltpu.VMEM((n, 8, 128), jnp.int32),
            pltpu.VMEM((blocks, tokens, 128), bf16),
            pltpu.VMEM((128, 128), bf16),
            pltpu.VMEM((unit * 128, tokens), jnp.float32),
            pltpu.VMEM((rows, heads * HEAD_SIZE), bf16),
            swap, swap, swap, swap,
            dma((2 * kv_heads + 2,)), dma((n,)), dma((n,)),
            dma((2 * kv_heads, n, 3)), dma((2 * kv_heads, n)),
            dma((groups, parts)), dma((groups, parts)), dma((groups, parts)), dma((groups, parts)),
        ],
        compiler_params=pltpu.CompilerParams(
            collective_id=0, has_side_effects=True, vmem_limit_bytes=60 * 2**20),
    )(queries, keys, values, out_weight, block_order)


def solution(mesh):
    n, tp = mesh.shape["ctx"], mesh.shape["tp"]
    in_specs = (P("ctx", "tp"), P("ctx", None), P("ctx", None), P("tp", None), P("ctx"))
    return jax.shard_map(functools.partial(shards, n, tp), mesh=mesh, in_specs=in_specs,
                         out_specs=P("ctx", "tp"), check_vma=False)
```

time: 192 us -> 73.7 us (0.38)
  waiting for transfers between devices: 92.6 us -> 0 us
  Pallas kernels: 0 us -> 71.7 us
  matrix products: 30.2 us -> 0 us
  local copies, waits for them, and re-layouts: 24.3 us -> 1.87 us
  between operations: 13.9 us -> 0.01 us
  blocking collectives: 13.1 us -> 0 us
  other arithmetic: 11.9 us -> 0 us
  loops' own time: 5.26 us -> 0 us
    pallas_call x0 -> x1, Pallas kernels: none -> 71.7 us  [shards(): pl.pallas_call(functools.partial(kernel, dims), out_shape=jax.ShapeDtypeS...]
    all_gather x2 -> x0, waiting for transfers between devices: 62.5 us -> none  [the longest x1 39.6 us: shards(): piece_values = lax.all_gather(own_values, 'ctx', axis=0, tiled=True)]
    dot_general x9 -> x0, matrix products: 30.2 us -> none  [the longest x4 12.6 us: update(): jnp.einsum('kgts,skd->tkgd', weights.astype(jnp.bfloat16), valued, prefer...]
    reduce_scatter x1 -> x0, waiting for transfers between devices: 30.1 us -> none  [shards(): lax.psum_scatter(lax.dot_general(out_weight, attended, (((0,), (1,)), (()...]
    unnamed x1 -> x0, blocking collectives: 13.1 us -> none
    unnamed x10 -> x1, local copies, waits for them, and re-layouts: 9.18 us -> 1.87 us
    reduce_sum x4 -> x0, other arithmetic: 6.79 us -> none  [update(): run_sum = run_sum * factor + jnp.sum(weights, axis=-1)]
    dynamic_slice x6 -> x0, local copies, waits for them, and re-layouts: 6.23 us -> none  [the longest x4 3.97 us: shards(): result, _ = lax.scan(advance, start_state, stacked)]
  transfers between devices with their start and end apart: 3 -> 0, of which waited for: 3 -> 0; matrix products, arithmetic and copies ran while one was open for 5% -> 0% of each run, Pallas kernels for 0% -> 0%
where the time goes in v1:
time: 73.7 us; the launch traced here: 73.5 us
  Pallas kernels  71.7 us (97%)
  local copies, waits for them, and re-layouts  1.87 us (3%)
    pallas_call x1, Pallas kernels, shards(): pl.pallas_call(functools.partial(kernel, dims), out_shape=jax.ShapeDtypeS...  71.7 us
    unnamed x1, local copies, waits for them, and re-layouts  1.87 us

profile of v1, /device:TPU:0, one launch (start us, length us, event | category | flops | bytes accessed | tf_op | source)
XLA Modules:
  0.0 73.5 jit_solution(1862669421862743726)
XLA Ops:
  0.0 71.7 %shard_map.55 = bf16[256,1024]{1,0:T(8,128)(2,1)} custom-call(bf16[256,2048]{1,0:T(8,128)(2,1)} %q_hbm.1, bf16[256,1024]{1,0:T(8,128)(2,1)} %k_hbm.1, bf16[256,1024]{1,0:T(8,128)(2,1)} %v_hbm.1, bf16[2048,4096]{1,0:T(8,128)(2,1)} %w_hbm.1, s32[2]{0:T(128)} %order.1), custom_call_target="tpu_custom_call" | custom-call | tf_op jit(solution)/shard_map/pallas_call | solution.py:277
  71.7 1.9 %copy.7 = bf16[256,1024]{1,0:T(8,128)(2,1)} copy(bf16[256,1024]{1,0:T(8,128)(2,1)} %shard_map.55) | data formatting | bytes 1048576

commit v2 on v1

--- a/solution.py
+++ b/solution.py
@@ -97,30 +97,39 @@
             if crossing:
                 piece(p, high, 2, a * 2 + other).start()
 
+    last = 2 * kv_heads - 1
+
     def step(h, s):
-        relay(2 * h, s, b, True)
-        relay(2 * h + 1, s, b, False)
-        relay(2 * h + 1, s, other, False)
+        for p in (2 * h, 2 * h + 1):
+            relay(p, s, b, p != last)
+            if p == last:
+                relay(p, s, other, False)
 
     def finish(h):
         def body(i, _):
-            piece(2 * h, i * 2 + other, 2, me).wait_recv()
+            for p in (2 * h, 2 * h + 1):
+                if p != last:
+                    piece(p, i * 2 + other, 2, me).wait_recv()
             return 0
         lax.fori_loop(0, line, body, 0)
 
-    for h in range(kv_heads):
-        for p in (2 * h, 2 * h + 1):
-            loads[p].wait()
-            open_line(p)
-        if h == 0:
-            for d in range(1, n):
-                order_copy(d, me, lax.rem(me + d, n)).start()
+    def open_own(p):
+        loads[p].wait()
+        open_line(p)
+
+    for d in range(1, n):
+        order_copy(d, me, lax.rem(me + d, n)).start()
+    for p in range(max(2, last)):
+        open_own(p)
     orders[pl.ds(me, 1)] = tile[...][None]
     row = lax.broadcasted_iota(jnp.int32, (128, 128), 0)
     col = lax.broadcasted_iota(jnp.int32, (128, 128), 1)
     eye[...] = (row == col).astype(jnp.bfloat16)
-    open_crossed(1)
-
+    if last == 1:
+        open_crossed(1)
+    step(0, 1)
+    if last > 1:
+        open_own(last)
     for d in range(1, n):
         order_copy(d, lax.rem(me + n - d, n), me).wait_recv()
 
@@ -134,7 +143,7 @@
         return 0
     lax.fori_loop(0, n, build, 0)
 
-    for s in range(1, line):
+    for s in range(2, line):
         step(0, s)
     finish(0)
     q_load.wait()
@@ -174,15 +183,20 @@
 
     total = blocks * per_block
     for h in range(kv_heads):
+        if h + 1 < kv_heads:
+            if 2 * h + 3 == last:
+                open_crossed(last)
+            step(h + 1, 1)
+
         def body(i, _):
             attend(h, i // per_block, lax.rem(i, per_block))
             if h + 1 < kv_heads:
-                guarded(i == 0, lambda: open_crossed(2 * h + 3))
-                guarded(jnp.logical_and(i > 0, i < line), lambda: step(h + 1, i))
+                s = (i + 3) // 2
+                guarded(jnp.logical_and(lax.rem(i, 2) == 1, s < line), lambda: step(h + 1, s))
             return 0
         lax.fori_loop(0, total, body, 0)
         if h + 1 < kv_heads:
-            for s in range(total, line):
+            for s in range(total // 2 + 2, line):
                 step(h + 1, s)
             finish(h + 1)
 
@@ -237,14 +251,14 @@
 
     def drain(i, _):
         for p in range(2 * kv_heads):
-            for side, tags in ((b, True), (other, p % 2 == 1)):
+            for side, tags in ((b, True), (other, p == last)):
                 blk = i * 2 + side
                 if tags:
                     guarded(jnp.logical_and(a + 1 < line, i <= a),
                             lambda: piece(p, blk, 0, me + 2).wait_send())
                     guarded(jnp.logical_and(a > 0, i >= a),
                             lambda: piece(p, blk, 1, me - 2).wait_send())
-            if p % 2 == 0:
+            if p != last:
                 piece(p, i * 2 + b, 2, a * 2 + other).wait_send()
             else:
                 guarded(i == a, lambda: piece(p, me, 2, a * 2 + other).wait_send())

time: 73.7 us -> 70.8 us (0.961)
  Pallas kernels: 71.7 us -> 68.8 us
    pallas_call x1, Pallas kernels: 71.7 us -> 68.8 us  [shards(): pl.pallas_call(functools.partial(kernel, dims), out_shape=jax.ShapeDtypeS...]
where the time goes in v2:
time: 70.8 us; the launch traced here: 70.6 us
  Pallas kernels  68.8 us (97%)
  local copies, waits for them, and re-layouts  1.87 us (3%)
    pallas_call x1, Pallas kernels, shards(): pl.pallas_call(functools.partial(kernel, dims), out_shape=jax.ShapeDtypeS...  68.8 us
    unnamed x1, local copies, waits for them, and re-layouts  1.87 us

profile of v2, /device:TPU:0, one launch (start us, length us, event | category | flops | bytes accessed | tf_op | source)
XLA Modules:
  0.0 70.6 jit_solution(6029534979268768026)
XLA Ops:
  0.0 68.8 %shard_map.55 = bf16[256,1024]{1,0:T(8,128)(2,1)} custom-call(bf16[256,2048]{1,0:T(8,128)(2,1)} %q_hbm.1, bf16[256,1024]{1,0:T(8,128)(2,1)} %k_hbm.1, bf16[256,1024]{1,0:T(8,128)(2,1)} %v_hbm.1, bf16[2048,4096]{1,0:T(8,128)(2,1)} %w_hbm.1, s32[2]{0:T(128)} %order.1), custom_call_target="tpu_custom_call" | custom-call | tf_op jit(solution)/shard_map/pallas_call | solution.py:291
  68.8 1.9 %copy.7 = bf16[256,1024]{1,0:T(8,128)(2,1)} copy(bf16[256,1024]{1,0:T(8,128)(2,1)} %shard_map.55) | data formatting | bytes 1048576

commit v3 on v1

--- a/solution.py
+++ b/solution.py
@@ -15,8 +15,8 @@
 NT = (((1,), (1,)), ((), ()))
 
 
-def kernel(dims, q_hbm, k_hbm, v_hbm, w_hbm, order, o_ref, q, w, kv, tile, orders, mask, eye, scores,
-           att, pair_out, pair_in, far_out, far_in, load_sem, order_send, order_recv, send, recv,
+def kernel(dims, q_hbm, k_hbm, v_hbm, w_hbm, order, o_ref, q, w, kv, orders, mask, eye, scores,
+           att, pair_out, pair_in, far_out, far_in, load_sem, send, recv,
            pair_send, pair_recv, far_send, far_recv):
     n, tp, rows, heads, kv_heads, unit, wide = dims
     line, groups = n // 2, tp // 2
@@ -45,97 +45,108 @@
     q_load.start()
     w_load.start()
     for i in range(blocks):
-        tile[pl.ds(i, 1), :] = jnp.full((1, 128), order[i], jnp.int32)
+        orders[pl.ds(me, 1), i:i + 1, :] = jnp.full((1, 1, 128), order[i], jnp.int32)
+
+    def guarded(cond, act):
+        pl.when(cond)(act)
+
+    up, down, across = a + 1 < line, a > 0, a * 2 + other
 
     barrier = pltpu.get_barrier_semaphore()
-    for d in range(1, n):
-        pl.semaphore_signal(barrier, inc=1, device_id=(lax.rem(me + d, n), t), device_id_type=MESH)
-    pl.semaphore_signal(barrier, inc=1, device_id=partner, device_id_type=MESH)
+
+    def greet(target):
+        pl.semaphore_signal(barrier, inc=1, device_id=target, device_id_type=MESH)
+
+    guarded(up, lambda: greet((me + 2, t)))
+    guarded(down, lambda: greet((me - 2, t)))
+    greet((across, t))
+    greet(partner)
     for i in range(1, groups):
-        pl.semaphore_signal(barrier, inc=1, device_id=(me, far(i) * 2 + c), device_id_type=MESH)
-    pl.semaphore_wait(barrier, n - 1 + 1 + groups - 1)
-
-    def order_copy(d, src_dev, target):
-        return pltpu.make_async_remote_copy(
-            src_ref=tile, dst_ref=orders.at[src_dev], send_sem=order_send.at[d],
-            recv_sem=order_recv.at[d], device_id=(target, t), device_id_type=MESH)
+        greet((me, far(i) * 2 + c))
+    pl.semaphore_wait(barrier, 1 + groups + up.astype(jnp.int32) + down.astype(jnp.int32))
+
+    marks = 2 * kv_heads
 
     def piece(p, block, way, target):
         at = pl.ds(pl.multiple_of(block * rows, 128), rows)
+        ref = orders.at[block] if p == marks else kv.at[p, at, :]
         return pltpu.make_async_remote_copy(
-            src_ref=kv.at[p, at, :], dst_ref=kv.at[p, at, :], send_sem=send.at[p, block, way],
+            src_ref=ref, dst_ref=ref, send_sem=send.at[p, block, way],
             recv_sem=recv.at[p, block], device_id=(target, t), device_id_type=MESH)
 
-    def guarded(cond, act):
-        pl.when(cond)(act)
-
-    def open_line(p):
-        guarded(a + 1 < line, lambda: piece(p, me, 0, me + 2).start())
-        guarded(a > 0, lambda: piece(p, me, 1, me - 2).start())
-        piece(p, me, 2, a * 2 + other).start()
-
-    def open_crossed(p):
-        blk = a * 2 + other
-        piece(p, blk, 2, blk).wait_recv()
-        guarded(a + 1 < line, lambda: piece(p, blk, 0, me + 2).start())
-        guarded(a > 0, lambda: piece(p, blk, 1, me - 2).start())
-
-    def relay(p, s, side, crossing):
-        low, high = (a - s) * 2 + side, (a + s) * 2 + side
+    def open_own(p):
+        if p != marks:
+            loads[p].wait()
+        guarded(up, lambda: piece(p, me, 0, me + 2).start())
+        guarded(down, lambda: piece(p, me, 1, me - 2).start())
+        piece(p, me, 2, across).start()
+
+    def relay(p, s):
+        low, high = me - 2 * s, me + 2 * s
 
         @pl.when(a - s >= 0)
         def _():
             piece(p, low, 0, me).wait_recv()
-            guarded(a + 1 < line, lambda: piece(p, low, 0, me + 2).start())
-            if crossing:
-                piece(p, low, 2, a * 2 + other).start()
+            guarded(up, lambda: piece(p, low, 0, me + 2).start())
+            piece(p, low, 2, across).start()
 
         @pl.when(a + s < line)
         def _():
             piece(p, high, 1, me).wait_recv()
-            guarded(a > 0, lambda: piece(p, high, 1, me - 2).start())
-            if crossing:
-                piece(p, high, 2, a * 2 + other).start()
+            guarded(down, lambda: piece(p, high, 1, me - 2).start())
+            piece(p, high, 2, across).start()
 
     def step(h, s):
-        relay(2 * h, s, b, True)
-        relay(2 * h + 1, s, b, False)
-        relay(2 * h + 1, s, other, False)
+        for p in (2 * h, 2 * h + 1):
+            relay(p, s)
 
     def finish(h):
         def body(i, _):
-            piece(2 * h, i * 2 + other, 2, me).wait_recv()
+            for p in (2 * h, 2 * h + 1):
+                piece(p, i * 2 + other, 2, me).wait_recv()
             return 0
         lax.fori_loop(0, line, body, 0)
 
-    for h in range(kv_heads):
-        for p in (2 * h, 2 * h + 1):
-            loads[p].wait()
-            open_line(p)
-        if h == 0:
-            for d in range(1, n):
-                order_copy(d, me, lax.rem(me + d, n)).start()
-    orders[pl.ds(me, 1)] = tile[...][None]
     row = lax.broadcasted_iota(jnp.int32, (128, 128), 0)
     col = lax.broadcasted_iota(jnp.int32, (128, 128), 1)
-    eye[...] = (row == col).astype(jnp.bfloat16)
-    open_crossed(1)
-
-    for d in range(1, n):
-        order_copy(d, lax.rem(me + n - d, n), me).wait_recv()
-
-    def build(i, _):
+
+    def build(i):
         for j in range(blocks):
             kpos = orders[pl.ds(i, 1), j:j + 1, :][0] * 128 + row
             for g in range(blocks):
-                qpos = tile[g:g + 1, :] * 128 + col
+                qpos = orders[pl.ds(me, 1), g:g + 1, :][0] * 128 + col
                 at = pl.ds(pl.multiple_of(i * rows + j * 128, 128), 128)
                 mask[g, at, :] = jnp.where(kpos <= qpos, 0.0, -1e30).astype(jnp.bfloat16)
-        return 0
-    lax.fori_loop(0, n, build, 0)
-
-    for s in range(1, line):
+
+    def build_crossed(s):
+        def one(i):
+            piece(marks, i, 2, me).wait_recv()
+            build(i)
+        guarded(a - s >= 0, lambda: one(across - 2 * s))
+        guarded(jnp.logical_and(s > 0, a + s < line), lambda: one(across + 2 * s))
+
+    open_own(marks)
+    early = min(3, 2 * kv_heads)
+    for p in range(early):
+        open_own(p)
+    eye[...] = (row == col).astype(jnp.bfloat16)
+    build(me)
+
+    def first_head(s, _):
+        relay(marks, s)
         step(0, s)
+        if kv_heads > 1:
+            @pl.when(s == 1)
+            def _():
+                for p in range(early, 2 * kv_heads):
+                    open_own(p)
+            guarded(s > 1, lambda: step(1, s - 1))
+        guarded(a - s >= 0, lambda: build(me - 2 * s))
+        guarded(a + s < line, lambda: build(me + 2 * s))
+        build_crossed(s - 1)
+        return 0
+    lax.fori_loop(1, line, first_head, 0)
+    build_crossed(jnp.int32(line - 1))
     finish(0)
     q_load.wait()
 
@@ -176,13 +187,12 @@
     for h in range(kv_heads):
         def body(i, _):
             attend(h, i // per_block, lax.rem(i, per_block))
-            if h + 1 < kv_heads:
-                guarded(i == 0, lambda: open_crossed(2 * h + 3))
-                guarded(jnp.logical_and(i > 0, i < line), lambda: step(h + 1, i))
+            if h == 0 and kv_heads > 1:
+                guarded(i == 1, lambda: step(1, line - 1))
             return 0
         lax.fori_loop(0, total, body, 0)
         if h + 1 < kv_heads:
-            for s in range(total, line):
+            for s in range(1 if h else line - 1, line) if (h or total < 2) else ():
                 step(h + 1, s)
             finish(h + 1)
 
@@ -232,22 +242,12 @@
         return 0
     lax.fori_loop(0, parts, close_step, 0)
 
-    for d in range(1, n):
-        order_copy(d, me, lax.rem(me + d, n)).wait_send()
-
     def drain(i, _):
-        for p in range(2 * kv_heads):
-            for side, tags in ((b, True), (other, p % 2 == 1)):
-                blk = i * 2 + side
-                if tags:
-                    guarded(jnp.logical_and(a + 1 < line, i <= a),
-                            lambda: piece(p, blk, 0, me + 2).wait_send())
-                    guarded(jnp.logical_and(a > 0, i >= a),
-                            lambda: piece(p, blk, 1, me - 2).wait_send())
-            if p % 2 == 0:
-                piece(p, i * 2 + b, 2, a * 2 + other).wait_send()
-            else:
-                guarded(i == a, lambda: piece(p, me, 2, a * 2 + other).wait_send())
+        for p in range(2 * kv_heads + 1):
+            blk = i * 2 + b
+            guarded(jnp.logical_and(up, i <= a), lambda: piece(p, blk, 0, me + 2).wait_send())
+            guarded(jnp.logical_and(down, i >= a), lambda: piece(p, blk, 1, me - 2).wait_send())
+            piece(p, blk, 2, across).wait_send()
         return 0
     lax.fori_loop(0, line, drain, 0)
 
@@ -283,15 +283,14 @@
             pltpu.VMEM(queries.shape, bf16),
             pltpu.VMEM(out_weight.shape, bf16),
             pltpu.VMEM((2 * kv_heads, tokens, HEAD_SIZE), bf16),
-            pltpu.VMEM((8, 128), jnp.int32),
             pltpu.VMEM((n, 8, 128), jnp.int32),
             pltpu.VMEM((blocks, tokens, 128), bf16),
             pltpu.VMEM((128, 128), bf16),
             pltpu.VMEM((unit * 128, tokens), jnp.float32),
             pltpu.VMEM((rows, heads * HEAD_SIZE), bf16),
             swap, swap, swap, swap,
-            dma((2 * kv_heads + 2,)), dma((n,)), dma((n,)),
-            dma((2 * kv_heads, n, 3)), dma((2 * kv_heads, n)),
+            dma((2 * kv_heads + 2,)),
+            dma((2 * kv_heads + 1, n, 3)), dma((2 * kv_heads + 1, n)),
             dma((groups, parts)), dma((groups, parts)), dma((groups, parts)), dma((groups, parts)),
         ],
         compiler_params=pltpu.CompilerParams(

time: 73.7 us -> 67.8 us (0.920)
  Pallas kernels: 71.7 us -> 65.7 us
    pallas_call x1, Pallas kernels: 71.7 us -> 65.7 us  [shards(): pl.pallas_call(functools.partial(kernel, dims), out_shape=jax.ShapeDtypeS...]
where the time goes in v3:
time: 67.8 us; the launch traced here: 67.6 us
  Pallas kernels  65.7 us (97%)
  local copies, waits for them, and re-layouts  1.87 us (3%)
    pallas_call x1, Pallas kernels, shards(): pl.pallas_call(functools.partial(kernel, dims), out_shape=jax.ShapeDtypeS...  65.7 us
    unnamed x1, local copies, waits for them, and re-layouts  1.87 us

profile of v3, /device:TPU:0, one launch (start us, length us, event | category | flops | bytes accessed | tf_op | source)
XLA Modules:
  0.0 67.6 jit_solution(8178026752584858239)
XLA Ops:
  0.0 65.7 %shard_map.55 = bf16[256,1024]{1,0:T(8,128)(2,1)} custom-call(bf16[256,2048]{1,0:T(8,128)(2,1)} %q_hbm.1, bf16[256,1024]{1,0:T(8,128)(2,1)} %k_hbm.1, bf16[256,1024]{1,0:T(8,128)(2,1)} %v_hbm.1, bf16[2048,4096]{1,0:T(8,128)(2,1)} %w_hbm.1, s32[2]{0:T(128)} %order.1), custom_call_target="tpu_custom_call" | custom-call | tf_op jit(solution)/shard_map/pallas_call | solution.py:277
  65.8 1.9 %copy.7 = bf16[256,1024]{1,0:T(8,128)(2,1)} copy(bf16[256,1024]{1,0:T(8,128)(2,1)} %shard_map.55) | data formatting | bytes 1048576

commit v4 on v3

--- a/solution.py
+++ b/solution.py
@@ -74,31 +74,42 @@
             src_ref=ref, dst_ref=ref, send_sem=send.at[p, block, way],
             recv_sem=recv.at[p, block], device_id=(target, t), device_id_type=MESH)
 
-    def open_own(p):
+    def open_own(p, crossing=True):
         if p != marks:
             loads[p].wait()
         guarded(up, lambda: piece(p, me, 0, me + 2).start())
         guarded(down, lambda: piece(p, me, 1, me - 2).start())
-        piece(p, me, 2, across).start()
-
-    def relay(p, s):
+        if crossing:
+            piece(p, me, 2, across).start()
+
+    def relay(p, s, crossing=True):
         low, high = me - 2 * s, me + 2 * s
 
         @pl.when(a - s >= 0)
         def _():
             piece(p, low, 0, me).wait_recv()
             guarded(up, lambda: piece(p, low, 0, me + 2).start())
-            piece(p, low, 2, across).start()
+            if crossing:
+                piece(p, low, 2, across).start()
 
         @pl.when(a + s < line)
         def _():
             piece(p, high, 1, me).wait_recv()
             guarded(down, lambda: piece(p, high, 1, me - 2).start())
-            piece(p, high, 2, across).start()
-
-    def step(h, s):
+            if crossing:
+                piece(p, high, 2, across).start()
+
+    def step(h, s, crossing=True):
         for p in (2 * h, 2 * h + 1):
-            relay(p, s)
+            relay(p, s, crossing)
+
+    def cross_held(h):
+        for p in (2 * h, 2 * h + 1):
+            piece(p, me, 2, across).start()
+        for s in range(1, line - 1):
+            for p in (2 * h, 2 * h + 1):
+                guarded(a - s >= 0, lambda: piece(p, me - 2 * s, 2, across).start())
+                guarded(a + s < line, lambda: piece(p, me + 2 * s, 2, across).start())
 
     def finish(h):
         def body(i, _):
@@ -126,9 +137,9 @@
         guarded(jnp.logical_and(s > 0, a + s < line), lambda: one(across + 2 * s))
 
     open_own(marks)
-    early = min(3, 2 * kv_heads)
+    early = 2 if line > 2 else 2 * kv_heads
     for p in range(early):
-        open_own(p)
+        open_own(p, p // 2 != 1)
     eye[...] = (row == col).astype(jnp.bfloat16)
     build(me)
 
@@ -136,18 +147,21 @@
         relay(marks, s)
         step(0, s)
         if kv_heads > 1:
-            @pl.when(s == 1)
-            def _():
-                for p in range(early, 2 * kv_heads):
-                    open_own(p)
-            guarded(s > 1, lambda: step(1, s - 1))
+            for p in range(early, 2 * kv_heads):
+                guarded(s == min(p - 1, 2), lambda p=p: open_own(p, p // 2 != 1))
         guarded(a - s >= 0, lambda: build(me - 2 * s))
         guarded(a + s < line, lambda: build(me + 2 * s))
         build_crossed(s - 1)
         return 0
     lax.fori_loop(1, line, first_head, 0)
+    if kv_heads > 1 and line > 2:
+        step(1, 1, False)
     build_crossed(jnp.int32(line - 1))
     finish(0)
+    if kv_heads > 1:
+        for s in range(2, line - 1):
+            step(1, s, False)
+        cross_held(1)
     q_load.wait()
 
     chunk = tokens // 4
@@ -188,7 +202,7 @@
         def body(i, _):
             attend(h, i // per_block, lax.rem(i, per_block))
             if h == 0 and kv_heads > 1:
-                guarded(i == 1, lambda: step(1, line - 1))
+                guarded(i == 0, lambda: step(1, line - 1))
             return 0
         lax.fori_loop(0, total, body, 0)
         if h + 1 < kv_heads:
@@ -265,7 +279,7 @@
     heads = queries.shape[1] // HEAD_SIZE
     group = QUERY_HEADS // KEY_VALUE_HEADS
     kv_heads = max(1, heads // group)
-    unit = min(2, heads // kv_heads)
+    unit = min(4, heads // kv_heads)
     quarter = out_weight.shape[1] // tp
     wide = min(256, quarter)
     parts, groups, tokens, blocks = quarter // wide, tp // 2, n * rows, rows // 128

time: 67.8 us -> 63.6 us (0.938)
  Pallas kernels: 65.7 us -> 61.5 us
    pallas_call x1, Pallas kernels: 65.7 us -> 61.5 us  [shards(): pl.pallas_call(functools.partial(kernel, dims), out_shape=jax.ShapeDtypeS...]
where the time goes in v4:
time: 63.6 us; the launch traced here: 63.4 us
  Pallas kernels  61.5 us (97%)
  local copies, waits for them, and re-layouts  1.87 us (3%)
    pallas_call x1, Pallas kernels, shards(): pl.pallas_call(functools.partial(kernel, dims), out_shape=jax.ShapeDtypeS...  61.5 us
    unnamed x1, local copies, waits for them, and re-layouts  1.87 us

profile of v4, /device:TPU:0, one launch (start us, length us, event | category | flops | bytes accessed | tf_op | source)
XLA Modules:
  0.0 63.4 jit_solution(15526998074216808224)
XLA Ops:
  0.0 61.5 %shard_map.55 = bf16[256,1024]{1,0:T(8,128)(2,1)} custom-call(bf16[256,2048]{1,0:T(8,128)(2,1)} %q_hbm.1, bf16[256,1024]{1,0:T(8,128)(2,1)} %k_hbm.1, bf16[256,1024]{1,0:T(8,128)(2,1)} %v_hbm.1, bf16[2048,4096]{1,0:T(8,128)(2,1)} %w_hbm.1, s32[2]{0:T(128)} %order.1), custom_call_target="tpu_custom_call" | custom-call | tf_op jit(solution)/shard_map/pallas_call | solution.py:291
  61.5 1.9 %copy.7 = bf16[256,1024]{1,0:T(8,128)(2,1)} copy(bf16[256,1024]{1,0:T(8,128)(2,1)} %shard_map.55) | data formatting | bytes 1048576

commit v5 on v3

--- a/solution.py
+++ b/solution.py
@@ -126,7 +126,7 @@
         guarded(jnp.logical_and(s > 0, a + s < line), lambda: one(across + 2 * s))
 
     open_own(marks)
-    early = min(3, 2 * kv_heads)
+    early = 2 if line > 2 else 2 * kv_heads
     for p in range(early):
         open_own(p)
     eye[...] = (row == col).astype(jnp.bfloat16)
@@ -136,18 +136,20 @@
         relay(marks, s)
         step(0, s)
         if kv_heads > 1:
-            @pl.when(s == 1)
-            def _():
-                for p in range(early, 2 * kv_heads):
-                    open_own(p)
-            guarded(s > 1, lambda: step(1, s - 1))
+            for p in range(early, 2 * kv_heads):
+                guarded(s == min(p - 1, 2), lambda p=p: open_own(p))
         guarded(a - s >= 0, lambda: build(me - 2 * s))
         guarded(a + s < line, lambda: build(me + 2 * s))
         build_crossed(s - 1)
         return 0
     lax.fori_loop(1, line, first_head, 0)
+    if kv_heads > 1 and line > 2:
+        step(1, 1)
     build_crossed(jnp.int32(line - 1))
     finish(0)
+    if kv_heads > 1:
+        for s in range(2, line - 1):
+            step(1, s)
     q_load.wait()
 
     chunk = tokens // 4
@@ -188,7 +190,7 @@
         def body(i, _):
             attend(h, i // per_block, lax.rem(i, per_block))
             if h == 0 and kv_heads > 1:
-                guarded(i == 1, lambda: step(1, line - 1))
+                guarded(i == 0, lambda: step(1, line - 1))
             return 0
         lax.fori_loop(0, total, body, 0)
         if h + 1 < kv_heads:
@@ -265,7 +267,7 @@
     heads = queries.shape[1] // HEAD_SIZE
     group = QUERY_HEADS // KEY_VALUE_HEADS
     kv_heads = max(1, heads // group)
-    unit = min(2, heads // kv_heads)
+    unit = min(4, heads // kv_heads)
     quarter = out_weight.shape[1] // tp
     wide = min(256, quarter)
     parts, groups, tokens, blocks = quarter // wide, tp // 2, n * rows, rows // 128

time: 67.8 us -> 63.3 us (0.934)
  Pallas kernels: 65.7 us -> 61.3 us
    pallas_call x1, Pallas kernels: 65.7 us -> 61.3 us  [shards(): pl.pallas_call(functools.partial(kernel, dims), out_shape=jax.ShapeDtypeS...]
where the time goes in v5:
time: 63.3 us; the launch traced here: 63.1 us
  Pallas kernels  61.3 us (97%)
  local copies, waits for them, and re-layouts  1.87 us (3%)
    pallas_call x1, Pallas kernels, shards(): pl.pallas_call(functools.partial(kernel, dims), out_shape=jax.ShapeDtypeS...  61.3 us
    unnamed x1, local copies, waits for them, and re-layouts  1.87 us

profile of v5, /device:TPU:0, one launch (start us, length us, event | category | flops | bytes accessed | tf_op | source)
XLA Modules:
  0.0 63.1 jit_solution(9213495131322085448)
XLA Ops:
  0.0 61.3 %shard_map.55 = bf16[256,1024]{1,0:T(8,128)(2,1)} custom-call(bf16[256,2048]{1,0:T(8,128)(2,1)} %q_hbm.1, bf16[256,1024]{1,0:T(8,128)(2,1)} %k_hbm.1, bf16[256,1024]{1,0:T(8,128)(2,1)} %v_hbm.1, bf16[2048,4096]{1,0:T(8,128)(2,1)} %w_hbm.1, s32[2]{0:T(128)} %order.1), custom_call_target="tpu_custom_call" | custom-call | tf_op jit(solution)/shard_map/pallas_call | solution.py:279
  61.3 1.9 %copy.7 = bf16[256,1024]{1,0:T(8,128)(2,1)} copy(bf16[256,1024]{1,0:T(8,128)(2,1)} %shard_map.55) | data formatting | bytes 1048576
